TPU v7x, 32 devices: a whole 2x2x4 slice. The times are simulated.
32 devices in a mesh: dp: 16 (over z, y, x), tensor: 2 (over core).
Axes of the slice: x: 2, y: 2, z: 4, core: 2. Of those that a mesh axis runs over, the one named last changes fastest.
Arguments:
- residual: bfloat16 [512, 6144], P('dp', 'tensor'), may hold values from -16 to 16
- queries: bfloat16 [512, 6144], P('dp', 'tensor'), may hold values from -4.5 to 4.5
- keys: bfloat16 [512, 128, 1024], P('dp', None, 'tensor'), may hold values from -4.5 to 4.5
- values: bfloat16 [512, 128, 1024], P('dp', None, 'tensor'), may hold values from -6 to 6
- lengths: int32 [512], P('dp'), may hold values from 2 to 128
- norm_gain: bfloat16 [6144], P('tensor'), may hold values from 0.099609375 to 1.8984375
- expert_ids: int32 [512, 2], P('dp'), may hold values from 0 to 7, all different within a row; in each aligned block of 32 rows (0 to 31, 32 to 63, ...) at most 16 rows name the same one
- expert_weights: float32 [512, 2], P('dp'), may hold values from 0.2 to 1
- w_in: bfloat16 [6144, 65536], P('tensor', 'dp'), may hold values from -0.078125 to 0.078125
- w_out: bfloat16 [65536, 6144], P('dp', 'tensor'), may hold values from -0.0625 to 0.0625
Outputs:
- output: bfloat16 [512, 6144], P('dp', 'tensor')
Inputs may be any that keep to these rules, and one draw needn't show every extreme that they name: `expert_ids`: each token names 2 different experts; at most 16 of the tokens of one index of dp name one expert, and in every draw some expert is named by exactly 16 of them.
All inputs are finite; a program needn't handle non-finite values.
Results may differ from a plain program's by a relative error of at most 0.008.
Values may be sent and summed in bfloat16 or wider, within the bound.
A program may use at most 128 MiB of HBM per device.

v0:
```python
import jax
import jax.numpy as jnp
from jax import lax
from jax.sharding import PartitionSpec as P

D = 6144
HEADS = 48
KV = 8
HEAD = 128
EXPERTS = 8
TOPK = 2
CACHE = 128
SRC_CAP = 16
NORM_EPSILON = 1e-05


def prefix(part, axis, combine, identity):
    place = lax.axis_index(axis)
    gathered = lax.all_gather(part, axis)
    state = jnp.zeros_like(part) + jnp.asarray(identity, part.dtype)

    def one(lap, state):
        return combine(state, lax.dynamic_index_in_dim(gathered, lap, 0, False))

    return lax.fori_loop(0, place, one, state)


def add_counts(earlier, later):
    return earlier + later


def expert_rows(tok_rows, w_in, w_out):
    partial_sum = jnp.einsum("df,rd->fr", w_in, tok_rows, preferred_element_type=jnp.float32)
    hidden_total = lax.psum(partial_sum.astype(jnp.bfloat16), "tensor").astype(jnp.float32)
    hidden = jax.nn.silu(hidden_total).astype(jnp.bfloat16)
    return jnp.einsum("fr,fd->rd", hidden, w_out, preferred_element_type=jnp.float32)


def shards(
    residual, queries, keys, values, lengths, norm_gain, expert_ids, expert_weights, w_in, w_out
):
    tokens = residual.shape[0]
    width_local = residual.shape[1]
    head_groups = keys.shape[2] // HEAD
    group_size = HEADS // KV
    query_rows = queries.reshape(tokens, head_groups, group_size, HEAD)
    key_rows = keys.reshape(tokens, CACHE, head_groups, HEAD)
    value_rows = values.reshape(tokens, CACHE, head_groups, HEAD)
    scores = jnp.einsum(
        "tgjd,tlgd->tgjl", query_rows, key_rows, preferred_element_type=jnp.float32
    ) * HEAD ** (-0.5)
    live_mask = (jnp.arange(CACHE, dtype=jnp.int32)[None, :] < lengths[:, None])[:, None, None, :]
    scores = jnp.where(live_mask, scores, -1e30)
    peak_score = jnp.max(scores, axis=-1, keepdims=True)
    powered = jnp.exp(scores - peak_score)
    attention_probs = (powered / jnp.sum(powered, axis=-1, keepdims=True)).astype(jnp.bfloat16)
    attended = jnp.einsum(
        "tgjl,tlgd->tgjd", attention_probs, value_rows, preferred_element_type=jnp.float32
    )
    summed = residual.astype(jnp.float32) + attended.reshape(tokens, width_local)
    square_sums = lax.psum(jnp.sum(summed * summed, axis=1), "tensor")
    normed = (
        summed
        * lax.rsqrt(square_sums[:, None] / D + NORM_EPSILON)
        * norm_gain.astype(jnp.float32)[None, :]
    ).astype(jnp.bfloat16)
    flat_ids = expert_ids.reshape(-1)
    expert_iota = jnp.arange(EXPERTS, dtype=jnp.int32)
    onehot = (flat_ids[:, None] == expert_iota[None, :]).astype(jnp.int32)
    local_rank = jnp.sum(
        (jnp.cumsum(onehot, axis=0, dtype=jnp.int32) - onehot) * onehot, axis=1, dtype=jnp.int32
    )
    counts = jnp.sum(onehot, axis=0, dtype=jnp.int32)
    offsets = prefix(counts, "dp", add_counts, jnp.zeros_like(counts))
    slot_index = local_rank + jnp.sum(onehot * offsets[None, :], axis=1, dtype=jnp.int32)
    capacity = tokens * lax.axis_size("dp") * TOPK * 3 // (4 * EXPERTS)
    keep_mask = slot_index < capacity
    owners = lax.axis_size("dp") // EXPERTS
    slot_total = EXPERTS * SRC_CAP
    pair_target = flat_ids * SRC_CAP + local_rank
    pick_pairs = pair_target[None, :] == jnp.arange(slot_total, dtype=jnp.int32)[:, None]
    pick_tokens = jnp.sum(
        pick_pairs.reshape(slot_total, tokens, TOPK).astype(jnp.float32), axis=2
    ).astype(jnp.bfloat16)
    packed = jnp.dot(pick_tokens, normed, preferred_element_type=jnp.float32).astype(jnp.bfloat16)
    outgoing = jnp.broadcast_to(
        packed.reshape(EXPERTS, 1, SRC_CAP, width_local), (EXPERTS, owners, SRC_CAP, width_local)
    )
    outgoing = outgoing.reshape(EXPERTS * owners, SRC_CAP, width_local)
    received = lax.all_to_all(outgoing, "dp", split_axis=0, concat_axis=0, tiled=True)
    total_rows = received.shape[0] * received.shape[1]
    results = expert_rows(received.reshape(total_rows, width_local), w_in, w_out)
    returned = results.reshape(received.shape[0], SRC_CAP, width_local)
    combined = lax.all_to_all(
        returned.astype(jnp.bfloat16), "dp", split_axis=0, concat_axis=0, tiled=True
    ).astype(returned.dtype)
    per_expert = jnp.sum(combined.reshape(EXPERTS, owners, SRC_CAP, width_local), axis=1).reshape(
        slot_total, width_local
    )
    pair_weight = expert_weights.reshape(-1) * keep_mask.astype(jnp.float32)
    mix_rows = jnp.sum(
        (pick_pairs.astype(jnp.float32) * pair_weight[None, :]).reshape(slot_total, tokens, TOPK),
        axis=2,
    )
    addition = jnp.einsum("st,sd->td", mix_rows, per_expert, precision=lax.Precision.HIGHEST)
    return (summed + addition).astype(jnp.bfloat16)


def solution(mesh):
    in_specs = (
        P("dp", "tensor"),
        P("dp", "tensor"),
        P("dp", None, "tensor"),
        P("dp", None, "tensor"),
        P("dp"),
        P("tensor"),
        P("dp", None),
        P("dp", None),
        P("tensor", "dp"),
        P("dp", "tensor"),
    )
    out_specs = P("dp", "tensor")
    return jax.shard_map(shards, mesh=mesh, in_specs=in_specs, out_specs=out_specs, check_vma=False)
```

profile of v0, /device:TPU:0, one launch (start us, length us, event | category | flops | bytes accessed | tf_op | source)
XLA Modules:
  0.0 180.8 jit_solution(6086627197087808506)
XLA Ops:
  6.5 0.0 all-reduce.3.cloned.1.call-start
  6.5 0.8 copy.37
  7.3 0.1 eq.30
  7.4 0.1 fusion.27
  7.5 0.1 fusion.26
  7.6 0.7 iota_compare_fusion.2
  8.3 0.7 convert_element_type.53
  9.0 1.2 dynamic-slice
  10.8 0.2 dynamic-update-slice
  11.1 16.2 %all-reduce = s32[128]{0:T(128)S(1)} all-reduce(s32[128]{0:T(128)S(1)} %dynamic-update-slice), channel_id=2, replica_groups=mesh['dp'=16,'tensor'=2] {'dp'}, use_global_device_ids=true, to_apply=%add | all-reduce | flops 128 | bytes 1024
  27.3 0.1 reshape.113
  27.4 0.1 reduce_window_sum.11
  27.5 0.2 select_reduce_fusion.1
  27.6 0.1 reduce_sum.81
  27.7 0.1 copy.40
  27.8 0.1 reduce_sum.78
  27.9 0.1 copy.38
  28.0 0.7 multiply_add_fusion
  28.7 1.2 reshape.102
  29.9 4.6 %fusion.30 = (f32[32,4,6]{2,1,0:T(4,128)S(1)}, f32[32,4,6,128]{3,2,1,0:T(8,128)S(1)}) fusion(bf16[32,4,6,128]{3,2,1,0:T(8,128)(2,1)S(1)} %reshape.102, pred[32,128]{1,0:T(8,128)(4,1)S(1)} %iota_compare_fusion.2, bf16[32,128,512]{2,1,0:T(8,128)(2,1)} %param.14), kind=kOutput, calls=%fused_computation.47 | convolution fusion | flops 25559168 | bytes 4791296 | tf_op jit(solution)/shard_map/sub | solution.py:55
  34.5 0.0 copy-start
  34.6 0.0 copy-start.1
  34.6 3.5 %fusion.6 = f32[32,4,6,128]{3,2,1,0:T(8,128)S(1)} fusion(f32[32,4,6,128]{3,2,1,0:T(8,128)S(1)} %get-tuple-element.42, f32[32,4,6]{2,1,0:T(4,128)S(1)} %get-tuple-element.41, bf16[32,128,512]{2,1,0:T(8,128)(2,1)} %param.15), kind=kOutput, calls=%fused_computation.10 | convolution fusion | flops 25362432 | bytes 4983808 | tf_op jit(solution)/shard_map/tgjl,tlgd->tgjd/dot_general | solution.py:57
  38.0 0.1 reshape.105
  38.2 0.0 copy-done
  38.2 0.2 multiply_reduce_fusion
  38.3 2.5 %psum.14 = f32[32]{0:T(128)S(1)} all-reduce(f32[32]{0:T(128)S(1)} %multiply_reduce_fusion), channel_id=1, replica_groups=mesh['dp'=16,'tensor'=2] {'tensor'}, use_global_device_ids=true, to_apply=%region_11.12 | all-reduce | flops 32 | bytes 256 | tf_op jit(solution)/shard_map/psum | solution.py:61
  40.8 0.0 copy-done.1
  40.8 0.1 convert_reduce_fusion.1
  40.9 0.4 convolution_convert_fusion.2
  41.3 0.2 broadcast_in_dim.19
  41.5 40.8 %all_to_all.10 = bf16[16,16,3072]{2,1,0:T(8,128)(2,1)S(1)} all-to-all(bf16[16,16,3072]{2,1,0:T(8,128)(2,1)S(1)} %bitcast.44), channel_id=1, replica_groups=mesh['dp'=16,'tensor'=2] {'dp'}, dimensions={0} | all-to-all | bytes 3145728 | tf_op jit(solution)/shard_map/all_to_all | solution.py:90
  82.3 13.2 %fusion.1 = bf16[4096,256]{0,1:T(8,128)(2,1)} fusion(bf16[256,3072]{1,0:T(8,128)(2,1)S(1)} %bitcast.46, bf16[3072,4096]{1,0:T(8,128)(2,1)} %param.20), kind=kOutput, calls=%fused_computation.5 | convolution fusion | flops 6443499520 | bytes 28835840 | tf_op jit(solution)/shard_map/df,rd->fr/dot_general | solution.py:33
  95.5 0.0 all-reduce.3.cloned.1.call-update
  95.5 19.7 %all-reduce.3.cloned.1.call-done = bf16[4096,256]{0,1:T(8,128)(2,1)} async-done(((bf16[4096,256]{0,1:T(8,128)(2,1)}), bf16[4096,256]{0,1:T(8,128)(2,1)}) %all-reduce.3.cloned.1.call-update) | async-done | bytes 2097168 | tf_op jit(solution)/shard_map/psum | solution.py:34
  115.3 12.2 %convolution_convert_fusion.1 = bf16[256,3072]{1,0:T(8,128)(2,1)S(1)} fusion(bf16[4096,3072]{1,0:T(8,128)(2,1)} %param.21, bf16[4096,256]{0,1:T(8,128)(2,1)} %all-reduce.3.cloned.1.call-done), kind=kOutput, calls=%fused_computation.16 | convolution fusion | flops 6449528832 | bytes 28835840 | tf_op jit(solution)/shard_map/fr,fd->rd/dot_general | solution.py:36
  127.5 44.6 %all_to_all.11 = bf16[16,16,3072]{2,1,0:T(8,128)(2,1)S(1)} all-to-all(bf16[16,16,3072]{2,1,0:T(8,128)(2,1)S(1)} %bitcast.47), channel_id=1, replica_groups=mesh['dp'=16,'tensor'=2] {'dp'}, dimensions={0} | all-to-all | bytes 3145728 | tf_op jit(solution)/shard_map/all_to_all | solution.py:94
  172.0 0.3 convert_reduce_fusion
  172.4 1.6 fusion.12
  (5 shorter events, 0.0 us)
Async XLA Ops:
  6.5 108.7 %all-reduce.3.cloned.1.call-start = ((), (), s32[]{:S(2)}) async-start(), calls=%async_computation.2 | async-start | bytes 4194304 | tf_op jit(solution)/shard_map/psum | solution.py:34
  34.5 3.6 %copy-start = (bf16[32,3072]{1,0:T(8,128)(2,1)S(1)}, bf16[32,3072]{1,0:T(8,128)(2,1)}, u32[]{:S(2)}) copy-start(bf16[32,3072]{1,0:T(8,128)(2,1)} %param.12) | copy-start | bytes 589828
  34.6 6.2 %copy-start.1 = (f32[32,2]{0,1:T(2,128)S(1)}, f32[32,2]{0,1:T(2,128)}, u32[]{:S(2)}) copy-start(f32[32,2]{0,1:T(2,128)} %param.19) | copy-start | bytes 772
Sparse Core Ops, SparseCore 0:
  95.6 19.5 all-reduce.2
where the time goes:
time: 181 us
  blocking collectives  104 us (57%)
  matrix products  35.5 us (20%)
  waiting for transfers between devices  19.8 us (11%)
  between operations  14.1 us (8%)
  local copies, waits for them, and re-layouts  4.26 us (2%)
  other arithmetic  3.15 us (2%)
    all_to_all x1, blocking collectives, shards(): lax.all_to_all(returned.astype(jnp.bfloat16), 'dp', split_axis=0, concat_...  44.6 us
    all_to_all x1, blocking collectives, shards(): lax.all_to_all(outgoing, 'dp', split_axis=0, concat_axis=0, tiled=True)  40.8 us
    psum x1, waiting for transfers between devices, expert_rows(): lax.psum(partial_sum.astype(jnp.bfloat16), 'tensor').astype(jnp.float32)  19.7 us
    unnamed x1, blocking collectives  16.2 us
    dot_general x1, matrix products, expert_rows(): jnp.einsum('df,rd->fr', w_in, tok_rows, preferred_element_type=jnp.float32)  13.2 us
    dot_general x1, matrix products, expert_rows(): jnp.einsum('fr,fd->rd', hidden, w_out, preferred_element_type=jnp.float32)  12.2 us
    sub x1, matrix products, shards(): powered = jnp.exp(scores - peak_score)  4.65 us
  transfers between devices with their start and end apart: 1, of which 1 were waited for; matrix products, arithmetic and copies ran while one was open for 0% of the time, Pallas kernels for 0%

commit v1 on v0

--- a/solution.py
+++ b/solution.py
@@ -31,7 +31,9 @@
 
 def expert_rows(tok_rows, w_in, w_out):
     partial_sum = jnp.einsum("df,rd->fr", w_in, tok_rows, preferred_element_type=jnp.float32)
-    hidden_total = lax.psum(partial_sum.astype(jnp.bfloat16), "tensor").astype(jnp.float32)
+    hidden_total = jnp.sum(
+        lax.all_gather(partial_sum.astype(jnp.bfloat16), "tensor"), axis=0
+    ).astype(jnp.float32)
     hidden = jax.nn.silu(hidden_total).astype(jnp.bfloat16)
     return jnp.einsum("fr,fd->rd", hidden, w_out, preferred_element_type=jnp.float32)
 

time: 181 us -> 193 us (1.066)
  other arithmetic: 3.15 us -> 14.9 us
  local copies, waits for them, and re-layouts: 4.26 us -> 12.1 us
  waiting for transfers between devices: 19.8 us -> 12.1 us
    psum x1 -> x0, waiting for transfers between devices: 19.7 us -> none  [expert_rows(): lax.psum(partial_sum.astype(jnp.bfloat16), 'tensor').astype(jnp.float32)]
    all_gather x0 -> x1, waiting for transfers between devices: none -> 12.1 us  [expert_rows(): lax.all_gather(partial_sum.astype(jnp.bfloat16), 'tensor')]
    reduce_sum x0 -> x1, other arithmetic: none -> 11.7 us  [expert_rows(): jnp.sum(lax.all_gather(partial_sum.astype(jnp.bfloat16), 'tensor'), axis=0)]
    all_gather x0 -> x1, local copies, waits for them, and re-layouts: none -> 7.8 us  [expert_rows(): lax.all_gather(partial_sum.astype(jnp.bfloat16), 'tensor')]
where the time goes in v1:
time: 193 us; the launch traced here: 192 us
  blocking collectives  104 us (54%)
  matrix products  35.3 us (18%)
  other arithmetic  14.9 us (8%)
  between operations  14.1 us (7%)
  local copies, waits for them, and re-layouts  12.1 us (6%)
  waiting for transfers between devices  12.1 us (6%)
    all_to_all x1, blocking collectives, shards(): lax.all_to_all(returned.astype(jnp.bfloat16), 'dp', split_axis=0, concat_...  44.5 us
    all_to_all x1, blocking collectives, shards(): lax.all_to_all(outgoing, 'dp', split_axis=0, concat_axis=0, tiled=True)  40.8 us
    unnamed x1, blocking collectives  16.2 us
    dot_general x1, matrix products, expert_rows(): jnp.einsum('df,rd->fr', w_in, tok_rows, preferred_element_type=jnp.float32)  13.2 us
    all_gather x1, waiting for transfers between devices, expert_rows(): lax.all_gather(partial_sum.astype(jnp.bfloat16), 'tensor')  12.1 us
    dot_general x1, matrix products, expert_rows(): jnp.einsum('fr,fd->rd', hidden, w_out, preferred_element_type=jnp.float32)  11.9 us
    reduce_sum x1, other arithmetic, expert_rows(): jnp.sum(lax.all_gather(partial_sum.astype(jnp.bfloat16), 'tensor'), axis=0)  11.7 us
    all_gather x1, local copies, waits for them, and re-layouts, expert_rows(): lax.all_gather(partial_sum.astype(jnp.bfloat16), 'tensor')  7.8 us
  transfers between devices with their start and end apart: 1, of which 1 were waited for; matrix products, arithmetic and copies ran while one was open for 0% of the time, Pallas kernels for 0%

profile of v1, /device:TPU:0, one launch (start us, length us, event | category | flops | bytes accessed | tf_op | source)
XLA Modules:
  0.0 192.4 jit_solution(11840857165363939411)
XLA Ops:
  6.5 0.0 all-gather.4.cloned.1.call-start
  6.5 0.8 copy.45
  7.3 0.1 eq.30
  7.4 0.1 fusion.27
  7.5 0.1 fusion.26
  7.6 0.7 iota_compare_fusion.2
  8.3 0.7 convert_element_type.55
  9.0 1.2 dynamic-slice
  10.8 0.2 dynamic-update-slice
  11.1 16.2 %all-reduce = s32[128]{0:T(128)S(1)} all-reduce(s32[128]{0:T(128)S(1)} %dynamic-update-slice), channel_id=2, replica_groups=mesh['dp'=16,'tensor'=2] {'dp'}, use_global_device_ids=true, to_apply=%add | all-reduce | flops 128 | bytes 1024
  27.3 0.1 reshape.113
  27.4 0.1 reduce_window_sum.11
  27.5 0.2 select_reduce_fusion.1
  27.6 0.1 reduce_sum.93
  27.7 0.1 copy.48
  27.8 0.1 reduce_sum.90
  27.9 0.1 copy.46
  28.0 0.7 multiply_add_fusion
  28.7 1.2 reshape.102
  29.9 4.6 %fusion.30 = (f32[32,4,6]{2,1,0:T(4,128)S(1)}, f32[32,4,6,128]{3,2,1,0:T(8,128)S(1)}) fusion(bf16[32,4,6,128]{3,2,1,0:T(8,128)(2,1)S(1)} %reshape.102, pred[32,128]{1,0:T(8,128)(4,1)S(1)} %iota_compare_fusion.2, bf16[32,128,512]{2,1,0:T(8,128)(2,1)} %param.14), kind=kOutput, calls=%fused_computation.47 | convolution fusion | flops 25559168 | bytes 4791296 | tf_op jit(solution)/shard_map/sub | solution.py:57
  34.5 0.0 copy-start
  34.6 0.0 copy-start.1
  34.6 3.5 %fusion.6 = f32[32,4,6,128]{3,2,1,0:T(8,128)S(1)} fusion(f32[32,4,6,128]{3,2,1,0:T(8,128)S(1)} %get-tuple-element.42, f32[32,4,6]{2,1,0:T(4,128)S(1)} %get-tuple-element.41, bf16[32,128,512]{2,1,0:T(8,128)(2,1)} %param.15), kind=kOutput, calls=%fused_computation.10 | convolution fusion | flops 25362432 | bytes 4983808 | tf_op jit(solution)/shard_map/tgjl,tlgd->tgjd/dot_general | solution.py:59
  38.0 0.1 reshape.105
  38.2 0.0 copy-done
  38.2 0.2 multiply_reduce_fusion
  38.3 2.5 %psum.7 = f32[32]{0:T(128)S(1)} all-reduce(f32[32]{0:T(128)S(1)} %multiply_reduce_fusion), channel_id=1, replica_groups=mesh['dp'=16,'tensor'=2] {'tensor'}, use_global_device_ids=true, to_apply=%region_11.12 | all-reduce | flops 32 | bytes 256 | tf_op jit(solution)/shard_map/psum | solution.py:63
  40.8 0.0 copy-done.1
  40.8 0.1 convert_reduce_fusion.1
  40.9 0.4 convolution_convert_fusion.2
  41.3 0.2 broadcast_in_dim.19
  41.5 40.8 %all_to_all.10 = bf16[16,16,3072]{2,1,0:T(8,128)(2,1)S(1)} all-to-all(bf16[16,16,3072]{2,1,0:T(8,128)(2,1)S(1)} %bitcast.46), channel_id=1, replica_groups=mesh['dp'=16,'tensor'=2] {'dp'}, dimensions={0} | all-to-all | bytes 3145728 | tf_op jit(solution)/shard_map/all_to_all | solution.py:92
  82.3 13.2 %fusion.1 = bf16[4096,256]{0,1:T(8,128)(2,1)} fusion(bf16[256,3072]{1,0:T(8,128)(2,1)S(1)} %bitcast.48, bf16[3072,4096]{1,0:T(8,128)(2,1)} %param.20), kind=kOutput, calls=%fused_computation.5 | convolution fusion | flops 6443499520 | bytes 28835840 | tf_op jit(solution)/shard_map/df,rd->fr/dot_general | solution.py:33
  95.5 0.0 all-gather.4.cloned.1.call-update
  95.6 12.1 %all-gather.4.cloned.1.call-done = bf16[8192,256]{0,1:T(8,128)(2,1)} async-done(((bf16[4096,256]{0,1:T(8,128)(2,1)}), bf16[8192,256]{0,1:T(8,128)(2,1)}) %all-gather.4.cloned.1.call-update) | async-done | bytes 4194320 | tf_op jit(solution)/shard_map/all_gather | solution.py:35
  107.6 7.8 %reshape.114 = bf16[2,4096,256]{1,0,2:T(2,128)(2,1)} reshape(bf16[8192,256]{0,1:T(8,128)(2,1)} %all-gather.4.cloned.1.call-done) | data formatting | bytes 8388608 | tf_op jit(solution)/shard_map/all_gather | solution.py:35
  115.5 11.7 %reduce_sum.97 = bf16[4096,256]{0,1:T(8,128)(2,1)S(1)} reduce(bf16[2,4096,256]{1,0,2:T(2,128)(2,1)} %reshape.114, bf16[]{:T(256)} %constant.44.clone.1), dimensions={0}, to_apply=%region_12.13 | reduce | flops 1048576 | bytes 6291458 | tf_op jit(solution)/shard_map/reduce_sum | solution.py:34
  127.2 11.9 %convolution_convert_fusion.1 = bf16[256,3072]{1,0:T(8,128)(2,1)S(1)} fusion(bf16[4096,3072]{1,0:T(8,128)(2,1)} %param.21, bf16[4096,256]{0,1:T(8,128)(2,1)S(1)} %reduce_sum.97), kind=kOutput, calls=%fused_computation.16 | convolution fusion | flops 6449528832 | bytes 28835840 | tf_op jit(solution)/shard_map/fr,fd->rd/dot_general | solution.py:38
  139.1 44.5 %all_to_all.11 = bf16[16,16,3072]{2,1,0:T(8,128)(2,1)S(1)} all-to-all(bf16[16,16,3072]{2,1,0:T(8,128)(2,1)S(1)} %bitcast.49), channel_id=1, replica_groups=mesh['dp'=16,'tensor'=2] {'dp'}, dimensions={0} | all-to-all | bytes 3145728 | tf_op jit(solution)/shard_map/all_to_all | solution.py:96
  183.6 0.3 convert_reduce_fusion
  184.0 1.6 fusion.12
  (5 shorter events, 0.0 us)
Async XLA Ops:
  6.5 101.1 %all-gather.4.cloned.1.call-start = ((), (), s32[]{:S(2)}) async-start(), calls=%async_computation.2 | async-start | bytes 6291456 | tf_op jit(solution)/shard_map/all_gather | solution.py:35
  34.5 3.6 %copy-start = (bf16[32,3072]{1,0:T(8,128)(2,1)S(1)}, bf16[32,3072]{1,0:T(8,128)(2,1)}, u32[]{:S(2)}) copy-start(bf16[32,3072]{1,0:T(8,128)(2,1)} %param.12) | copy-start | bytes 589828
  34.6 6.2 %copy-start.1 = (f32[32,2]{0,1:T(2,128)S(1)}, f32[32,2]{0,1:T(2,128)}, u32[]{:S(2)}) copy-start(f32[32,2]{0,1:T(2,128)} %param.19) | copy-start | bytes 772
Sparse Core Ops, SparseCore 0:
  95.7 11.9 all-gather.3
